TPU v7x, 32 devices: a whole 2x2x4 slice. The times are simulated.
32 devices in a mesh: band: 2 (over x), row: 16 (over z, y, core).
Axes of the slice: x: 2, y: 2, z: 4, core: 2. Of those that a mesh axis runs over, the one named last changes fastest.
Arguments:
- shot_traces: bfloat16 [16384, 4096], P(('band', 'row')), parts along dimension 0, may hold values from -6 to 6
- source_cell: int32 [16384], P(('band', 'row')), parts along dimension 0, may hold values from 0 to 127
- receiver_cell: int32 [16384], P(('band', 'row')), parts along dimension 0, may hold values from 0 to 127
- band_order: int32 [64], P('band'), parts along dimension 0, may hold values from 0 to 31, each once
Outputs:
- next_grid: float32 [64, 2, 128, 128], P(('band', 'row')), parts along dimension 0
There are 2 independent parts, one for each index of `band`. A program takes and returns all parts, laid end to end along the dimension named above; each array names one. Nothing has to cross between parts.
Inputs may be any that keep to these rules, and one draw needn't show every extreme that they name: `band_order`: a permutation of 0 to 31.
All inputs are finite; a program needn't handle non-finite values.
Results may differ from a plain program's by a relative error of at most 0.0037.
Values may be sent and summed in bfloat16 or wider, within the bound.
A program may use at most 64 MiB of HBM per device.

v0:
```python
import math

import jax
import jax.numpy as jnp
from jax import lax
from jax.sharding import PartitionSpec as P

FLO = 64
SC = 128
RC = 128


def local(shot_traces, source_cell, receiver_cell, band_order):
    samples_count = shot_traces.shape[1]
    band_size = band_order.shape[0]
    local_traces = shot_traces.shape[0]
    bins = FLO + band_order
    samples = jnp.arange(samples_count, dtype=jnp.int32)
    phase = samples[:, None] * bins[None, :] % samples_count
    angle = 2.0 * math.pi * phase.astype(jnp.float32) / samples_count
    scale = 1.0 / math.sqrt(samples_count)
    table = jnp.concatenate([jnp.cos(angle) * scale, -jnp.sin(angle) * scale], axis=1).astype(
        jnp.bfloat16
    )
    spectra = jnp.dot(shot_traces, table, preferred_element_type=jnp.float32).astype(jnp.bfloat16)
    spectra = spectra.reshape(local_traces, 2, band_size)
    source_range = jnp.arange(SC, dtype=jnp.float32)
    receiver_range = jnp.arange(RC, dtype=jnp.float32)
    cells = jnp.stack([source_cell, receiver_cell], axis=1).astype(jnp.bfloat16)
    cells = jnp.broadcast_to(cells[:, :, None], (local_traces, 2, band_size))
    packed = jnp.concatenate([spectra, cells], axis=1)
    moved = lax.all_to_all(packed, "row", split_axis=2, concat_axis=0, tiled=True)
    received = moved[:, 0:2, :]
    source_value = moved[:, 2, 0].astype(jnp.float32)
    receiver_value = moved[:, 3, 0].astype(jnp.float32)
    source_hot = (source_value[:, None] == source_range[None, :]).astype(jnp.bfloat16)
    receiver_hot = (receiver_value[:, None] == receiver_range[None, :]).astype(jnp.bfloat16)
    counts = jnp.einsum("ts,tr->sr", source_hot, receiver_hot, preferred_element_type=jnp.float32)
    weighted = received[:, :, :, None] * receiver_hot[:, None, None, :]
    stack = jnp.einsum("ts,tcfr->fcsr", source_hot, weighted, preferred_element_type=jnp.float32)
    next_grid = stack / jnp.maximum(counts, 1.0)[None, None, :, :]
    return next_grid


def solution(mesh):
    placed = (P(("band", "row"), None), P(("band", "row")), P(("band", "row")), P("band"))
    return jax.shard_map(
        local,
        mesh=mesh,
        in_specs=placed,
        out_specs=P(("band", "row"), None, None, None),
        check_vma=False,
    )
```

profile of v0, /device:TPU:0, one launch (start us, length us, event | category | flops | bytes accessed | tf_op | source)
XLA Modules:
  0.0 29.5 jit_solution(11736142359959002785)
XLA Ops:
  0.0 0.7 %broadcast_add_fusion = s32[32]{0:T(128)S(1)} fusion(s32[32]{0:T(128)} %param.7), kind=kLoop, calls=%fused_computation.36 | loop fusion | flops 32 | bytes 256 | tf_op jit(solution)/shard_map/add | solution.py:17
  0.7 0.7 %convert.18 = bf16[512]{0:T(512)(128)(2,1)S(1)} convert(s32[512]{0:T(512)} %param.5) | non-fusion elementwise | flops 512 | bytes 3072 | tf_op jit(solution)/shard_map/convert.5
  1.4 0.7 %convert.19 = bf16[512]{0:T(512)(128)(2,1)S(1)} convert(s32[512]{0:T(512)} %param.6) | non-fusion elementwise | flops 512 | bytes 3072 | tf_op jit(solution)/shard_map/convert.4
  2.0 2.5 %multiply_convert_fusion.1 = (bf16[4096,32]{0,1:T(8,128)(2,1)S(1)}, bf16[4096,32]{0,1:T(8,128)(2,1)S(1)}) fusion(s32[32]{0:T(128)S(1)} %broadcast_add_fusion), kind=kLoop, calls=%fused_computation.27 | loop fusion | flops 2490368 | bytes 524416 | tf_op jit(solution)/shard_map/convert.6
  4.5 3.6 %convolution_convert_fusion = bf16[64,512]{1,0:T(8,128)(2,1)S(1)} fusion(bf16[512,4096]{1,0:T(8,128)(2,1)} %param.4, bf16[4096,32]{0,1:T(8,128)(2,1)S(1)} %get-tuple-element.8, bf16[4096,32]{0,1:T(8,128)(2,1)S(1)} %get-tuple-element.7), kind=kOutput, calls=%fused_computation.14 | convolution fusion | flops 269516800 | bytes 4784128 | tf_op jit(solution)/shard_map/dot_general | solution.py:25
  8.1 0.1 copy.14
  8.3 0.1 pad_maximum_fusion
  8.4 15.1 %all_to_all.18 = bf16[512,4,32]{0,1,2:T(4,128)(2,1)S(1)} all-to-all(bf16[512,4,32]{0,1,2:T(4,128)(2,1)S(1)} %pad_maximum_fusion), channel_id=1, replica_groups=mesh['band'=2,'row'=16] {'row'}, dimensions={2} | all-to-all | bytes 262144 | tf_op jit(solution)/shard_map/all_to_all | solution.py:32
  23.6 0.1 all_to_all.16
  23.8 0.4 %fusion.6 = bf16[8192,128]{0,1:T(8,128)(2,1)S(1)} fusion(f32[8192]{0:T(1024)S(1)} %bitcast.30), kind=kLoop, calls=%fused_computation.8 | loop fusion | flops 2097152 | bytes 2129920 | tf_op jit(solution)/shard_map/convert_element_type | solution.py:37
  24.2 1.9 %fusion.18 = f32[128,128]{1,0:T(8,128)S(1)} fusion(f32[8192]{0:T(1024)S(1)} %bitcast.31, f32[8192]{0:T(1024)S(1)} %bitcast.32), kind=kOutput, calls=%fused_computation.15 | convolution fusion | flops 271597568 | bytes 131072 | tf_op jit(solution)/shard_map/ts,tr->sr/dot_general | solution.py:38
  26.2 0.1 copy.16
  26.2 2.4 %fusion.21 = f32[2,2,128,128]{2,3,0,1:T(8,128)S(1)} fusion(f32[8192]{0:T(1024)S(1)} %bitcast.33, bf16[8192,128]{0,1:T(8,128)(2,1)S(1)} %fusion.6, bf16[8192,2,2]{0,2,1:T(2,128)(2,1)S(1)} %slice.12, f32[128,128]{0,1:T(8,128)S(1)} %copy.16), kind=kOutput, calls=%fused_computation.16 | convolution fusion | flops 1079050240 | bytes 2523136 | tf_op jit(solution)/shard_map/ts,tcfr->fcsr/dot_general | solution.py:40
  28.7 0.8 %copy.17 = f32[2,2,128,128]{3,2,1,0:T(8,128)} copy(f32[2,2,128,128]{2,3,0,1:T(8,128)S(1)} %fusion.21) | data formatting | bytes 524288 | tf_op jit(solution)/shard_map/div | solution.py:41
  (7 shorter events, 0.2 us)
where the time goes:
time: 29.8 us; the launch traced here: 29.5 us
  blocking collectives  15.1 us (51%)
  matrix products  7.99 us (27%)
  other arithmetic  5.12 us (17%)
  local copies, waits for them, and re-layouts  1.22 us (4%)
    all_to_all x1, blocking collectives, local(): lax.all_to_all(packed, 'row', split_axis=2, concat_axis=0, tiled=True)  15.1 us
    another operation x3, other arithmetic  3.83 us
    dot_general x1, matrix products, local(): jnp.dot(shot_traces, table, preferred_element_type=jnp.float32)  3.6 us
    dot_general x1, matrix products, local(): jnp.einsum('ts,tcfr->fcsr', source_hot, weighted, preferred_element_type=...  2.45 us
    dot_general x1, matrix products, local(): jnp.einsum('ts,tr->sr', source_hot, receiver_hot, preferred_element_type=...  1.95 us
    div x1, local copies, waits for them, and re-layouts, local(): next_grid = stack / jnp.maximum(counts, 1.0)[None, None, :, :]  0.84 us
    add x1, other arithmetic, local(): bins = FLO + band_order  0.66 us

commit v1 on v0

v1 whole, which is shorter than its diff:
```python
import functools
import math

import jax
import jax.numpy as jnp
import ml_dtypes
import numpy as np
from jax import lax
from jax.experimental import pallas as pl
from jax.experimental.pallas import tpu as pltpu
from jax.sharding import PartitionSpec as P

FLO = 64
SC = 128
RC = 128
NCHUNK = 2
BF = jnp.bfloat16
F32 = jnp.float32
NT_DIMS = (((1,), (1,)), ((), ()))
TN_DIMS = (((0,), (0,)), ((), ()))


def natural_table(samples_count, band_size):
    bins = FLO + np.arange(band_size)
    phase = (bins[:, None] * np.arange(samples_count)[None, :]) % samples_count
    angle = 2.0 * math.pi * phase / samples_count
    scale = 1.0 / math.sqrt(samples_count)
    table = np.stack([np.cos(angle) * scale, -np.sin(angle) * scale], axis=1)
    return table.reshape(2 * band_size, samples_count).astype(np.float32).astype(ml_dtypes.bfloat16)


def kernel(
    n,
    traces_hbm,
    source_hbm,
    receiver_hbm,
    order_hbm,
    table_hbm,
    out_ref,
    traces,
    source,
    receiver,
    order,
    table,
    lhs,
    cells_out,
    cells_in,
    send,
    recv,
    source_hot,
    receiver_hot,
    counts,
    stack,
    load_sem,
    traces_sem,
    cell_send_sem,
    cell_recv_sem,
    send_sem,
    recv_sem,
    own_sem,
):
    me = lax.axis_index("row")
    chunk = traces.shape[1]
    rows, samples_count = table.shape
    channels = send.shape[2]

    def load(at, src, dst):
        return pltpu.make_async_copy(src, dst, load_sem.at[at])

    loads = [
        load(0, source_hbm, source),
        load(1, receiver_hbm, receiver),
        load(2, order_hbm, order),
        load(3, table_hbm, table),
    ]
    for copy in loads:
        copy.start()
    trace_loads = [
        pltpu.make_async_copy(
            traces_hbm.at[pl.ds(c * chunk, chunk)], traces.at[c], traces_sem.at[c]
        )
        for c in range(NCHUNK)
    ]
    for copy in trace_loads:
        copy.start()

    barrier = pltpu.get_barrier_semaphore()

    def greet(i, carry):
        pl.semaphore_signal(barrier, inc=1, device_id={"row": lax.rem(me + i, n)})
        return carry

    lax.fori_loop(1, n, greet, 0)

    loads[0].wait()
    loads[1].wait()
    cells_out[...] = source[...] * RC + receiver[...]

    loads[2].wait()
    band_size = rows // 2
    spread = (
        lax.broadcasted_iota(jnp.int32, (band_size, rows), 0)
        == lax.broadcasted_iota(jnp.int32, (band_size, rows), 1) // 2
    ).astype(BF)
    bins = jnp.broadcast_to(order[...].astype(F32), (8, band_size)).astype(BF)
    wanted = jnp.dot(bins, spread, preferred_element_type=F32)[0:1]
    part = lax.broadcasted_iota(jnp.int32, (1, rows), 1) % 2
    wanted = 2.0 * wanted + part.astype(F32)
    held = lax.broadcasted_iota(jnp.int32, (rows, rows), 0).astype(F32)
    pick = (held == wanted).astype(F32).astype(BF)
    loads[3].wait()
    for at in range(0, samples_count, 1024):
        cut = pl.ds(at, 1024)
        lhs[:, cut] = lax.dot_general(
            pick, table[:, cut], TN_DIMS, preferred_element_type=F32
        ).astype(BF)

    pl.semaphore_wait(barrier, n - 1)

    def cell_copy(peer, slot):
        return pltpu.make_async_remote_copy(
            src_ref=cells_out,
            dst_ref=cells_in.at[slot],
            send_sem=cell_send_sem.at[peer],
            recv_sem=cell_recv_sem.at[slot],
            device_id={"row": peer},
        )

    def send_cells(i, carry):
        cell_copy(lax.rem(me + i, n), me).start()
        return carry

    lax.fori_loop(1, n, send_cells, 0)
    own_cells = pltpu.make_async_copy(cells_out, cells_in.at[me], own_sem.at[NCHUNK])
    own_cells.start()

    def value_copy(c, peer, slot):
        return pltpu.make_async_remote_copy(
            src_ref=send.at[c, peer],
            dst_ref=recv.at[c, slot],
            send_sem=send_sem.at[c, peer],
            recv_sem=recv_sem.at[c, slot],
            device_id={"row": peer},
        )

    own_values = []
    for c in range(NCHUNK):
        trace_loads[c].wait()
        spectra = lax.dot_general(
            lhs[...], traces[c], NT_DIMS, preferred_element_type=F32
        )
        send[c] = spectra.reshape(n, channels, chunk).astype(BF)

        def send_values(i, carry, c=c):
            value_copy(c, lax.rem(me + i, n), me).start()
            return carry

        lax.fori_loop(1, n, send_values, 0)
        own = pltpu.make_async_copy(send.at[c, me], recv.at[c, me], own_sem.at[c])
        own.start()
        own_values.append(own)

    per_device = cells_out.shape[1]
    cell_at = lax.broadcasted_iota(jnp.int32, (SC, per_device), 0)
    counts[...] = jnp.zeros_like(counts)

    def hot(src):
        cell = cells_in[src]
        s_hot = (cell_at == cell // RC).astype(F32).astype(BF)
        r_hot = (cell_at == cell % RC).astype(F32).astype(BF)
        source_hot[src] = s_hot
        receiver_hot[src] = r_hot
        counts[...] += lax.dot_general(s_hot, r_hot, NT_DIMS, preferred_element_type=F32)

    own_cells.wait()
    hot(me)

    def hot_step(i, carry):
        src = lax.rem(me + n - i, n)
        cell_copy(src, src).wait_recv()
        hot(src)
        return carry

    lax.fori_loop(1, n, hot_step, 0)

    stack[...] = jnp.zeros_like(stack)

    def add(c, src):
        cut = pl.ds(c * chunk, chunk)
        s_hot = source_hot[src, :, cut]
        r_hot = receiver_hot[src, :, cut]
        values = recv[c, src]
        weighted = jnp.concatenate(
            [r_hot * values[m : m + 1, :] for m in range(channels)], axis=0
        )
        stack[...] += lax.dot_general(s_hot, weighted, NT_DIMS, preferred_element_type=F32)

    for c in range(NCHUNK):
        own_values[c].wait()
        add(c, me)

        def add_step(i, carry, c=c):
            src = lax.rem(me + n - i, n)
            value_copy(c, src, src).wait_recv()
            add(c, src)
            return carry

        lax.fori_loop(1, n, add_step, 0)

    scale = 1.0 / jnp.maximum(counts[...], 1.0)
    for m in range(channels):
        out_ref[m // 2, m % 2] = stack[:, m * RC : (m + 1) * RC] * scale

    def drain(i, carry):
        peer = lax.rem(me + i, n)
        cell_copy(peer, me).wait_send()
        for c in range(NCHUNK):
            value_copy(c, peer, me).wait_send()
        return carry

    lax.fori_loop(1, n, drain, 0)


def local(n, shot_traces, source_cell, receiver_cell, band_order):
    local_traces, samples_count = shot_traces.shape
    band_size = band_order.shape[0]
    own_slots = band_size // n
    rows = 2 * band_size
    channels = 2 * own_slots
    chunk = local_traces // NCHUNK
    table = jnp.asarray(natural_table(samples_count, band_size))
    anywhere = pl.BlockSpec(memory_space=pltpu.HBM)
    return pl.pallas_call(
        functools.partial(kernel, n),
        out_shape=jax.ShapeDtypeStruct((own_slots, 2, SC, RC), F32),
        in_specs=[anywhere] * 5,
        out_specs=pl.BlockSpec(memory_space=pltpu.VMEM),
        scratch_shapes=[
            pltpu.VMEM((NCHUNK, chunk, samples_count), BF),
            pltpu.VMEM((1, local_traces), jnp.int32),
            pltpu.VMEM((1, local_traces), jnp.int32),
            pltpu.VMEM((1, band_size), jnp.int32),
            pltpu.VMEM((rows, samples_count), BF),
            pltpu.VMEM((rows, samples_count), BF),
            pltpu.VMEM((1, local_traces), jnp.int32),
            pltpu.VMEM((n, 1, local_traces), jnp.int32),
            pltpu.VMEM((NCHUNK, n, channels, chunk), BF),
            pltpu.VMEM((NCHUNK, n, channels, chunk), BF),
            pltpu.VMEM((n, SC, local_traces), BF),
            pltpu.VMEM((n, RC, local_traces), BF),
            pltpu.VMEM((SC, RC), F32),
            pltpu.VMEM((SC, channels * RC), F32),
            pltpu.SemaphoreType.DMA((4,)),
            pltpu.SemaphoreType.DMA((NCHUNK,)),
            pltpu.SemaphoreType.DMA((n,)),
            pltpu.SemaphoreType.DMA((n,)),
            pltpu.SemaphoreType.DMA((NCHUNK, n)),
            pltpu.SemaphoreType.DMA((NCHUNK, n)),
            pltpu.SemaphoreType.DMA((NCHUNK + 1,)),
        ],
        compiler_params=pltpu.CompilerParams(
            collective_id=0, has_side_effects=True, vmem_limit_bytes=48 * 1024 * 1024
        ),
    )(
        shot_traces,
        source_cell.reshape(1, local_traces),
        receiver_cell.reshape(1, local_traces),
        band_order.reshape(1, band_size),
        table,
    )


def solution(mesh):
    placed = (P(("band", "row"), None), P(("band", "row")), P(("band", "row")), P("band"))
    return jax.shard_map(
        functools.partial(local, mesh.shape["row"]),
        mesh=mesh,
        in_specs=placed,
        out_specs=P(("band", "row"), None, None, None),
        check_vma=False,
    )
```

time: 29.8 us -> 27.6 us (0.926)
  Pallas kernels: 0 us -> 21.4 us
  blocking collectives: 15.1 us -> 0 us
  matrix products: 7.99 us -> 0 us
  other arithmetic: 5.12 us -> 0 us
  local copies, waits for them, and re-layouts: 1.22 us -> 5.95 us
    pallas_call x0 -> x1, Pallas kernels: none -> 21.4 us  [local(): pl.pallas_call(functools.partial(kernel, n), out_shape=jax.ShapeDtypeStru...]
    all_to_all x1 -> x0, blocking collectives: 15.1 us -> none  [local(): lax.all_to_all(packed, 'row', split_axis=2, concat_axis=0, tiled=True)]
    dot_general x3 -> x0, matrix products: 7.99 us -> none  [the longest x1 3.6 us: local(): jnp.dot(shot_traces, table, preferred_element_type=jnp.float32)]
    unnamed x0 -> x11, local copies, waits for them, and re-layouts: none -> 5.95 us
    another operation x4 -> x0, other arithmetic: 3.84 us -> none
    div x1 -> x0, local copies, waits for them, and re-layouts: 0.84 us -> none  [local(): next_grid = stack / jnp.maximum(counts, 1.0)[None, None, :, :]]
    add x1 -> x0, other arithmetic: 0.66 us -> none  [local(): bins = FLO + band_order]
    convert_element_type x2 -> x0, other arithmetic: 0.48 us -> none  [the longest x1 0.43 us: local(): (receiver_value[:, None] == receiver_range[None, :]).astype(jnp.bfloat16)]
where the time goes in v1:
time: 27.6 us; the launch traced here: 27.4 us
  Pallas kernels  21.4 us (78%)
  local copies, waits for them, and re-layouts  5.95 us (22%)
    pallas_call x1, Pallas kernels, local(): pl.pallas_call(functools.partial(kernel, n), out_shape=jax.ShapeDtypeStru...  21.4 us
    unnamed x11, local copies, waits for them, and re-layouts  5.95 us

profile of v1, /device:TPU:0, one launch (start us, length us, event | category | flops | bytes accessed | tf_op | source)
XLA Modules:
  0.0 27.4 jit_solution(7632581541171426877)
XLA Ops:
  0.0 0.0 copy-start
  0.0 2.2 %copy-done = bf16[512,4096]{1,0:T(8,128)(2,1)S(1)} copy-done((bf16[512,4096]{1,0:T(8,128)(2,1)S(1)}, bf16[512,4096]{1,0:T(8,128)(2,1)}, u32[]{:S(2)}) %copy-start) | copy-done | bytes 4194328
  2.2 0.0 copy-start.1
  2.2 1.0 %copy-done.1 = bf16[64,4096]{1,0:T(8,128)(2,1)S(1)} copy-done((bf16[64,4096]{1,0:T(8,128)(2,1)S(1)}, bf16[64,4096]{1,0:T(8,128)(2,1)}, u32[]{:S(2)}) %copy-start.1) | copy-done | bytes 524312
  3.2 0.0 copy-start.2
  3.2 0.7 %copy-done.2 = s32[512]{0:T(512)S(1)} copy-done((s32[512]{0:T(512)S(1)}, s32[512]{0:T(512)}, u32[]{:S(2)}) %copy-start.2) | copy-done | bytes 2072
  3.9 0.0 copy-start.3
  3.9 0.7 %copy-done.3 = s32[512]{0:T(512)S(1)} copy-done((s32[512]{0:T(512)S(1)}, s32[512]{0:T(512)}, u32[]{:S(2)}) %copy-start.3) | copy-done | bytes 2072
  4.6 0.0 copy-start.4
  4.6 0.7 %copy-done.4 = s32[32]{0:T(128)S(1)} copy-done((s32[32]{0:T(128)S(1)}, s32[32]{0:T(128)}, u32[]{:S(2)}) %copy-start.4) | copy-done | bytes 152
  5.3 21.4 %shard_map.55 = f32[2,2,128,128]{3,2,1,0:T(8,128)S(1)} custom-call(bf16[512,4096]{1,0:T(8,128)(2,1)S(1)} %copy-done, s32[1,512]{1,0:T(1,128)S(1)} %bitcast.3, s32[1,512]{1,0:T(1,128)S(1)} %bitcast.4, s32[1,32]{1,0:T(1,128)S(1)} %bitcast.5, bf16[64,4096]{1,0:T(8,128)(2,1)S(1)} %copy-done.1), custom_call_target="tpu_custom_call" | custom-call | tf_op jit(solution)/shard_map/pallas_call | solution.py:233
  26.7 0.7 %copy.7 = f32[2,2,128,128]{3,2,1,0:T(8,128)} copy(f32[2,2,128,128]{3,2,1,0:T(8,128)S(1)} %shard_map.55) | data formatting | bytes 524288
Async XLA Ops:
  0.0 2.2 %copy-start = (bf16[512,4096]{1,0:T(8,128)(2,1)S(1)}, bf16[512,4096]{1,0:T(8,128)(2,1)}, u32[]{:S(2)}) copy-start(bf16[512,4096]{1,0:T(8,128)(2,1)} %traces_hbm.1) | copy-start | bytes 12582916
  2.2 1.0 %copy-start.1 = (bf16[64,4096]{1,0:T(8,128)(2,1)S(1)}, bf16[64,4096]{1,0:T(8,128)(2,1)}, u32[]{:S(2)}) copy-start(bf16[64,4096]{1,0:T(8,128)(2,1)} %constant.2.clone.table_hbm) | copy-start | bytes 1572868
  3.2 0.7 %copy-start.2 = (s32[512]{0:T(512)S(1)}, s32[512]{0:T(512)}, u32[]{:S(2)}) copy-start(s32[512]{0:T(512)} %param.6) | copy-start | bytes 6148
  3.9 0.7 %copy-start.3 = (s32[512]{0:T(512)S(1)}, s32[512]{0:T(512)}, u32[]{:S(2)}) copy-start(s32[512]{0:T(512)} %param.7) | copy-start | bytes 6148
  4.6 0.7 %copy-start.4 = (s32[32]{0:T(128)S(1)}, s32[32]{0:T(128)}, u32[]{:S(2)}) copy-start(s32[32]{0:T(128)} %param.8) | copy-start | bytes 388

commit v2 on v1

--- a/solution.py
+++ b/solution.py
@@ -14,6 +14,7 @@
 SC = 128
 RC = 128
 NCHUNK = 2
+GROUP = 4
 BF = jnp.bfloat16
 F32 = jnp.float32
 NT_DIMS = (((1,), (1,)), ((), ()))
@@ -47,9 +48,6 @@
     cells_in,
     send,
     recv,
-    source_hot,
-    receiver_hot,
-    counts,
     stack,
     load_sem,
     traces_sem,
@@ -115,8 +113,6 @@
             pick, table[:, cut], TN_DIMS, preferred_element_type=F32
         ).astype(BF)
 
-    pl.semaphore_wait(barrier, n - 1)
-
     def cell_copy(peer, slot):
         return pltpu.make_async_remote_copy(
             src_ref=cells_out,
@@ -126,14 +122,6 @@
             device_id={"row": peer},
         )
 
-    def send_cells(i, carry):
-        cell_copy(lax.rem(me + i, n), me).start()
-        return carry
-
-    lax.fori_loop(1, n, send_cells, 0)
-    own_cells = pltpu.make_async_copy(cells_out, cells_in.at[me], own_sem.at[NCHUNK])
-    own_cells.start()
-
     def value_copy(c, peer, slot):
         return pltpu.make_async_remote_copy(
             src_ref=send.at[c, peer],
@@ -151,6 +139,17 @@
         )
         send[c] = spectra.reshape(n, channels, chunk).astype(BF)
 
+        if c == 0:
+            pl.semaphore_wait(barrier, n - 1)
+
+            def send_cells(i, carry):
+                cell_copy(lax.rem(me + i, n), me).start()
+                return carry
+
+            lax.fori_loop(1, n, send_cells, 0)
+            own_cells = pltpu.make_async_copy(cells_out, cells_in.at[me], own_sem.at[NCHUNK])
+            own_cells.start()
+
         def send_values(i, carry, c=c):
             value_copy(c, lax.rem(me + i, n), me).start()
             return carry
@@ -160,54 +159,53 @@
         own.start()
         own_values.append(own)
 
-    per_device = cells_out.shape[1]
-    cell_at = lax.broadcasted_iota(jnp.int32, (SC, per_device), 0)
-    counts[...] = jnp.zeros_like(counts)
-
-    def hot(src):
-        cell = cells_in[src]
-        s_hot = (cell_at == cell // RC).astype(F32).astype(BF)
-        r_hot = (cell_at == cell % RC).astype(F32).astype(BF)
-        source_hot[src] = s_hot
-        receiver_hot[src] = r_hot
-        counts[...] += lax.dot_general(s_hot, r_hot, NT_DIMS, preferred_element_type=F32)
+    cell_at = lax.broadcasted_iota(jnp.int32, (SC, chunk), 0)
+    stack[...] = jnp.zeros_like(stack)
+
+    def add(sources):
+        s_parts, w_parts = [], []
+        for src in sources:
+            for c in range(NCHUNK):
+                cell = cells_in[src, :, c * chunk : (c + 1) * chunk]
+                s_parts.append((cell_at == cell // RC).astype(F32).astype(BF))
+                r_hot = (cell_at == cell % RC).astype(F32).astype(BF)
+                values = recv[c, src]
+                w_parts.append(
+                    jnp.concatenate(
+                        [r_hot * values[m : m + 1, :] for m in range(channels)] + [r_hot],
+                        axis=0,
+                    )
+                )
+        stack[...] += lax.dot_general(
+            jnp.concatenate(s_parts, axis=1),
+            jnp.concatenate(w_parts, axis=1),
+            NT_DIMS,
+            preferred_element_type=F32,
+        )
+
+    def arrive(src):
+        cell_copy(src, src).wait_recv()
+        for c in range(NCHUNK):
+            value_copy(c, src, src).wait_recv()
 
     own_cells.wait()
-    hot(me)
-
-    def hot_step(i, carry):
-        src = lax.rem(me + n - i, n)
-        cell_copy(src, src).wait_recv()
-        hot(src)
+    for own in own_values:
+        own.wait()
+    group = [lax.rem(me + n - k, n) for k in range(GROUP)]
+    for src in group[1:]:
+        arrive(src)
+    add(group)
+
+    def add_step(g, carry):
+        sources = [lax.rem(me + n - (g * GROUP + k), n) for k in range(GROUP)]
+        for src in sources:
+            arrive(src)
+        add(sources)
         return carry
 
-    lax.fori_loop(1, n, hot_step, 0)
-
-    stack[...] = jnp.zeros_like(stack)
-
-    def add(c, src):
-        cut = pl.ds(c * chunk, chunk)
-        s_hot = source_hot[src, :, cut]
-        r_hot = receiver_hot[src, :, cut]
-        values = recv[c, src]
-        weighted = jnp.concatenate(
-            [r_hot * values[m : m + 1, :] for m in range(channels)], axis=0
-        )
-        stack[...] += lax.dot_general(s_hot, weighted, NT_DIMS, preferred_element_type=F32)
-
-    for c in range(NCHUNK):
-        own_values[c].wait()
-        add(c, me)
-
-        def add_step(i, carry, c=c):
-            src = lax.rem(me + n - i, n)
-            value_copy(c, src, src).wait_recv()
-            add(c, src)
-            return carry
-
-        lax.fori_loop(1, n, add_step, 0)
-
-    scale = 1.0 / jnp.maximum(counts[...], 1.0)
+    lax.fori_loop(1, n // GROUP, add_step, 0)
+
+    scale = 1.0 / jnp.maximum(stack[:, channels * RC :], 1.0)
     for m in range(channels):
         out_ref[m // 2, m % 2] = stack[:, m * RC : (m + 1) * RC] * scale
 
@@ -246,10 +244,7 @@
             pltpu.VMEM((n, 1, local_traces), jnp.int32),
             pltpu.VMEM((NCHUNK, n, channels, chunk), BF),
             pltpu.VMEM((NCHUNK, n, channels, chunk), BF),
-            pltpu.VMEM((n, SC, local_traces), BF),
-            pltpu.VMEM((n, RC, local_traces), BF),
-            pltpu.VMEM((SC, RC), F32),
-            pltpu.VMEM((SC, channels * RC), F32),
+            pltpu.VMEM((SC, (channels + 1) * RC), F32),
             pltpu.SemaphoreType.DMA((4,)),
             pltpu.SemaphoreType.DMA((NCHUNK,)),
             pltpu.SemaphoreType.DMA((n,)),
@@ -259,7 +254,7 @@
             pltpu.SemaphoreType.DMA((NCHUNK + 1,)),
         ],
         compiler_params=pltpu.CompilerParams(
-            collective_id=0, has_side_effects=True, vmem_limit_bytes=48 * 1024 * 1024
+            collective_id=0, has_side_effects=True, vmem_limit_bytes=64 * 1024 * 1024 - 65536
         ),
     )(
         shot_traces,

time: 27.6 us -> 20.2 us (0.73)
  local copies, waits for them, and re-layouts: 5.95 us -> 1.67 us
  Pallas kernels: 21.4 us -> 18.3 us
    unnamed x11 -> x1, local copies, waits for them, and re-layouts: 5.95 us -> 1.67 us
    pallas_call x1, Pallas kernels: 21.4 us -> 18.3 us  [local(): pl.pallas_call(functools.partial(kernel, n), out_shape=jax.ShapeDtypeStru...]
where the time goes in v2:
time: 20.2 us; the launch traced here: 20 us
  Pallas kernels  18.3 us (91%)
  local copies, waits for them, and re-layouts  1.67 us (8%)
    pallas_call x1, Pallas kernels, local(): pl.pallas_call(functools.partial(kernel, n), out_shape=jax.ShapeDtypeStru...  18.3 us
    unnamed x1, local copies, waits for them, and re-layouts  1.67 us

profile of v2, /device:TPU:0, one launch (start us, length us, event | category | flops | bytes accessed | tf_op | source)
XLA Modules:
  0.0 20.0 jit_solution(14689670712766234162)
XLA Ops:
  0.0 18.3 %shard_map.55 = f32[2,2,128,128]{3,2,1,0:T(8,128)} custom-call(bf16[512,4096]{1,0:T(8,128)(2,1)} %traces_hbm.1, s32[1,512]{1,0:T(1,128)} %bitcast.3, s32[1,512]{1,0:T(1,128)} %bitcast.4, s32[1,32]{1,0:T(1,128)} %bitcast.5, bf16[64,4096]{1,0:T(8,128)(2,1)} %constant.2.clone.table_hbm), custom_call_target="tpu_custom_call" | custom-call | tf_op jit(solution)/shard_map/pallas_call | solution.py:231
  18.3 1.7 %copy.7 = f32[2,2,128,128]{3,2,1,0:T(8,128)} copy(f32[2,2,128,128]{3,2,1,0:T(8,128)} %shard_map.55) | data formatting | bytes 524288

commit v3 on v2

--- a/solution.py
+++ b/solution.py
@@ -230,7 +230,7 @@
     anywhere = pl.BlockSpec(memory_space=pltpu.HBM)
     return pl.pallas_call(
         functools.partial(kernel, n),
-        out_shape=jax.ShapeDtypeStruct((own_slots, 2, SC, RC), F32),
+        out_shape=pltpu.VMEM((own_slots, 2, SC, RC), F32),
         in_specs=[anywhere] * 5,
         out_specs=pl.BlockSpec(memory_space=pltpu.VMEM),
         scratch_shapes=[
@@ -254,7 +254,7 @@
             pltpu.SemaphoreType.DMA((NCHUNK + 1,)),
         ],
         compiler_params=pltpu.CompilerParams(
-            collective_id=0, has_side_effects=True, vmem_limit_bytes=64 * 1024 * 1024 - 65536
+            collective_id=0, has_side_effects=True, vmem_limit_bytes=64 * 1024 * 1024 - 65536 - 1024 * 1024
         ),
     )(
         shot_traces,

time: 20.2 us -> 18.5 us (0.916)
  local copies, waits for them, and re-layouts: 1.67 us -> 0.71 us
  Pallas kernels: 18.3 us -> 17.6 us
    unnamed x1, local copies, waits for them, and re-layouts: 1.67 us -> 0.71 us
    pallas_call x1, Pallas kernels: 18.3 us -> 17.6 us  [local(): pl.pallas_call(functools.partial(kernel, n), out_shape=pltpu.VMEM((own_sl...]
where the time goes in v3:
time: 18.5 us; the launch traced here: 18.3 us
  Pallas kernels  17.6 us (95%)
  local copies, waits for them, and re-layouts  0.71 us (4%)
    pallas_call x1, Pallas kernels, local(): pl.pallas_call(functools.partial(kernel, n), out_shape=pltpu.VMEM((own_sl...  17.6 us
    unnamed x1, local copies, waits for them, and re-layouts  0.71 us

profile of v3, /device:TPU:0, one launch (start us, length us, event | category | flops | bytes accessed | tf_op | source)
XLA Modules:
  0.0 18.3 jit_solution(16830087984868596867)
XLA Ops:
  0.0 17.6 %shard_map.55 = f32[2,2,128,128]{3,2,1,0:T(8,128)S(1)} custom-call(bf16[512,4096]{1,0:T(8,128)(2,1)} %traces_hbm.1, s32[1,512]{1,0:T(1,128)} %bitcast.3, s32[1,512]{1,0:T(1,128)} %bitcast.4, s32[1,32]{1,0:T(1,128)} %bitcast.5, bf16[64,4096]{1,0:T(8,128)(2,1)} %constant.2.clone.table_hbm), custom_call_target="tpu_custom_call" | custom-call | tf_op jit(solution)/shard_map/pallas_call | solution.py:231
  17.6 0.7 %copy.7 = f32[2,2,128,128]{3,2,1,0:T(8,128)} copy(f32[2,2,128,128]{3,2,1,0:T(8,128)S(1)} %shard_map.55) | data formatting | bytes 524288

commit v4 on v3

--- a/solution.py
+++ b/solution.py
@@ -13,7 +13,7 @@
 FLO = 64
 SC = 128
 RC = 128
-NCHUNK = 2
+PIECES = 8
 GROUP = 4
 BF = jnp.bfloat16
 F32 = jnp.float32
@@ -58,9 +58,10 @@
     own_sem,
 ):
     me = lax.axis_index("row")
-    chunk = traces.shape[1]
+    piece = traces.shape[2]
+    per_device = traces.shape[1]
     rows, samples_count = table.shape
-    channels = send.shape[2]
+    channels = send.shape[1]
 
     def load(at, src, dst):
         return pltpu.make_async_copy(src, dst, load_sem.at[at])
@@ -75,9 +76,9 @@
         copy.start()
     trace_loads = [
         pltpu.make_async_copy(
-            traces_hbm.at[pl.ds(c * chunk, chunk)], traces.at[c], traces_sem.at[c]
-        )
-        for c in range(NCHUNK)
+            traces_hbm.at[:, pl.ds(c * piece, piece)], traces.at[c], traces_sem.at[c]
+        )
+        for c in range(PIECES)
     ]
     for copy in trace_loads:
         copy.start()
@@ -122,24 +123,18 @@
             device_id={"row": peer},
         )
 
-    def value_copy(c, peer, slot):
+    def value_copy(peer, slot):
         return pltpu.make_async_remote_copy(
-            src_ref=send.at[c, peer],
-            dst_ref=recv.at[c, slot],
-            send_sem=send_sem.at[c, peer],
-            recv_sem=recv_sem.at[c, slot],
+            src_ref=send.at[peer],
+            dst_ref=recv.at[slot],
+            send_sem=send_sem.at[peer],
+            recv_sem=recv_sem.at[slot],
             device_id={"row": peer},
         )
 
-    own_values = []
-    for c in range(NCHUNK):
-        trace_loads[c].wait()
-        spectra = lax.dot_general(
-            lhs[...], traces[c], NT_DIMS, preferred_element_type=F32
-        )
-        send[c] = spectra.reshape(n, channels, chunk).astype(BF)
-
-        if c == 0:
+    spectra = jnp.zeros((rows, per_device), F32)
+    for c in range(PIECES):
+        if c == PIECES - 1:
             pl.semaphore_wait(barrier, n - 1)
 
             def send_cells(i, carry):
@@ -147,35 +142,41 @@
                 return carry
 
             lax.fori_loop(1, n, send_cells, 0)
-            own_cells = pltpu.make_async_copy(cells_out, cells_in.at[me], own_sem.at[NCHUNK])
+            own_cells = pltpu.make_async_copy(cells_out, cells_in.at[me], own_sem.at[0])
             own_cells.start()
-
-        def send_values(i, carry, c=c):
-            value_copy(c, lax.rem(me + i, n), me).start()
-            return carry
-
-        lax.fori_loop(1, n, send_values, 0)
-        own = pltpu.make_async_copy(send.at[c, me], recv.at[c, me], own_sem.at[c])
-        own.start()
-        own_values.append(own)
-
-    cell_at = lax.broadcasted_iota(jnp.int32, (SC, chunk), 0)
+        trace_loads[c].wait()
+        spectra += lax.dot_general(
+            lhs[:, c * piece : (c + 1) * piece],
+            traces[c],
+            NT_DIMS,
+            preferred_element_type=F32,
+        )
+    send[...] = spectra.reshape(n, channels, per_device).astype(BF)
+
+    def send_values(i, carry):
+        value_copy(lax.rem(me + i, n), me).start()
+        return carry
+
+    lax.fori_loop(1, n, send_values, 0)
+    own_values = pltpu.make_async_copy(send.at[me], recv.at[me], own_sem.at[1])
+    own_values.start()
+
+    cell_at = lax.broadcasted_iota(jnp.int32, (SC, per_device), 0)
     stack[...] = jnp.zeros_like(stack)
 
     def add(sources):
         s_parts, w_parts = [], []
         for src in sources:
-            for c in range(NCHUNK):
-                cell = cells_in[src, :, c * chunk : (c + 1) * chunk]
-                s_parts.append((cell_at == cell // RC).astype(F32).astype(BF))
-                r_hot = (cell_at == cell % RC).astype(F32).astype(BF)
-                values = recv[c, src]
-                w_parts.append(
-                    jnp.concatenate(
-                        [r_hot * values[m : m + 1, :] for m in range(channels)] + [r_hot],
-                        axis=0,
-                    )
+            cell = cells_in[src]
+            s_parts.append((cell_at == cell // RC).astype(F32).astype(BF))
+            r_hot = (cell_at == cell % RC).astype(F32).astype(BF)
+            values = recv[src]
+            w_parts.append(
+                jnp.concatenate(
+                    [r_hot * values[m : m + 1, :] for m in range(channels)] + [r_hot],
+                    axis=0,
                 )
+            )
         stack[...] += lax.dot_general(
             jnp.concatenate(s_parts, axis=1),
             jnp.concatenate(w_parts, axis=1),
@@ -183,27 +184,22 @@
             preferred_element_type=F32,
         )
 
-    def arrive(src):
-        cell_copy(src, src).wait_recv()
-        for c in range(NCHUNK):
-            value_copy(c, src, src).wait_recv()
-
     own_cells.wait()
-    for own in own_values:
-        own.wait()
-    group = [lax.rem(me + n - k, n) for k in range(GROUP)]
-    for src in group[1:]:
-        arrive(src)
-    add(group)
+    own_values.wait()
 
     def add_step(g, carry):
-        sources = [lax.rem(me + n - (g * GROUP + k), n) for k in range(GROUP)]
+        sources = [g * GROUP + k for k in range(GROUP)]
         for src in sources:
-            arrive(src)
+
+            @pl.when(src != me)
+            def _():
+                cell_copy(src, src).wait_recv()
+                value_copy(src, src).wait_recv()
+
         add(sources)
         return carry
 
-    lax.fori_loop(1, n // GROUP, add_step, 0)
+    lax.fori_loop(0, n // GROUP, add_step, 0)
 
     scale = 1.0 / jnp.maximum(stack[:, channels * RC :], 1.0)
     for m in range(channels):
@@ -212,8 +208,7 @@
     def drain(i, carry):
         peer = lax.rem(me + i, n)
         cell_copy(peer, me).wait_send()
-        for c in range(NCHUNK):
-            value_copy(c, peer, me).wait_send()
+        value_copy(peer, me).wait_send()
         return carry
 
     lax.fori_loop(1, n, drain, 0)
@@ -225,7 +220,7 @@
     own_slots = band_size // n
     rows = 2 * band_size
     channels = 2 * own_slots
-    chunk = local_traces // NCHUNK
+    piece = samples_count // PIECES
     table = jnp.asarray(natural_table(samples_count, band_size))
     anywhere = pl.BlockSpec(memory_space=pltpu.HBM)
     return pl.pallas_call(
@@ -234,7 +229,7 @@
         in_specs=[anywhere] * 5,
         out_specs=pl.BlockSpec(memory_space=pltpu.VMEM),
         scratch_shapes=[
-            pltpu.VMEM((NCHUNK, chunk, samples_count), BF),
+            pltpu.VMEM((PIECES, local_traces, piece), BF),
             pltpu.VMEM((1, local_traces), jnp.int32),
             pltpu.VMEM((1, local_traces), jnp.int32),
             pltpu.VMEM((1, band_size), jnp.int32),
@@ -242,16 +237,16 @@
             pltpu.VMEM((rows, samples_count), BF),
             pltpu.VMEM((1, local_traces), jnp.int32),
             pltpu.VMEM((n, 1, local_traces), jnp.int32),
-            pltpu.VMEM((NCHUNK, n, channels, chunk), BF),
-            pltpu.VMEM((NCHUNK, n, channels, chunk), BF),
+            pltpu.VMEM((n, channels, local_traces), BF),
+            pltpu.VMEM((n, channels, local_traces), BF),
             pltpu.VMEM((SC, (channels + 1) * RC), F32),
             pltpu.SemaphoreType.DMA((4,)),
-            pltpu.SemaphoreType.DMA((NCHUNK,)),
-            pltpu.SemaphoreType.DMA((n,)),
-            pltpu.SemaphoreType.DMA((n,)),
-            pltpu.SemaphoreType.DMA((NCHUNK, n)),
-            pltpu.SemaphoreType.DMA((NCHUNK, n)),
-            pltpu.SemaphoreType.DMA((NCHUNK + 1,)),
+            pltpu.SemaphoreType.DMA((PIECES,)),
+            pltpu.SemaphoreType.DMA((n,)),
+            pltpu.SemaphoreType.DMA((n,)),
+            pltpu.SemaphoreType.DMA((n,)),
+            pltpu.SemaphoreType.DMA((n,)),
+            pltpu.SemaphoreType.DMA((2,)),
         ],
         compiler_params=pltpu.CompilerParams(
             collective_id=0, has_side_effects=True, vmem_limit_bytes=64 * 1024 * 1024 - 65536 - 1024 * 1024

time: 18.5 us -> 14.7 us (0.79)
  Pallas kernels: 17.6 us -> 13.8 us
    pallas_call x1, Pallas kernels: 17.6 us -> 13.8 us  [local(): pl.pallas_call(functools.partial(kernel, n), out_shape=pltpu.VMEM((own_sl...]
where the time goes in v4:
time: 14.7 us; the launch traced here: 14.5 us
  Pallas kernels  13.8 us (94%)
  local copies, waits for them, and re-layouts  0.71 us (5%)
    pallas_call x1, Pallas kernels, local(): pl.pallas_call(functools.partial(kernel, n), out_shape=pltpu.VMEM((own_sl...  13.8 us
    unnamed x1, local copies, waits for them, and re-layouts  0.71 us

profile of v4, /device:TPU:0, one launch (start us, length us, event | category | flops | bytes accessed | tf_op | source)
XLA Modules:
  0.0 14.5 jit_solution(4596352623062144237)
XLA Ops:
  0.0 13.8 %shard_map.55 = f32[2,2,128,128]{3,2,1,0:T(8,128)S(1)} custom-call(bf16[512,4096]{1,0:T(8,128)(2,1)} %traces_hbm.1, s32[1,512]{1,0:T(1,128)} %bitcast.3, s32[1,512]{1,0:T(1,128)} %bitcast.4, s32[1,32]{1,0:T(1,128)} %bitcast.5, bf16[64,4096]{1,0:T(8,128)(2,1)} %constant.2.clone.table_hbm), custom_call_target="tpu_custom_call" | custom-call | tf_op jit(solution)/shard_map/pallas_call | solution.py:226
  13.8 0.7 %copy.7 = f32[2,2,128,128]{3,2,1,0:T(8,128)} copy(f32[2,2,128,128]{3,2,1,0:T(8,128)S(1)} %shard_map.55) | data formatting | bytes 524288

commit v5 on v4

--- a/solution.py
+++ b/solution.py
@@ -13,7 +13,7 @@
 FLO = 64
 SC = 128
 RC = 128
-PIECES = 8
+PIECES = 4
 GROUP = 4
 BF = jnp.bfloat16
 F32 = jnp.float32
@@ -161,25 +161,27 @@
     own_values = pltpu.make_async_copy(send.at[me], recv.at[me], own_sem.at[1])
     own_values.start()
 
-    cell_at = lax.broadcasted_iota(jnp.int32, (SC, per_device), 0)
+    cell_at = lax.broadcasted_iota(jnp.int32, (SC, per_device), 0).astype(F32).astype(BF)
+    one = jnp.ones((SC, per_device), BF)
+    none = jnp.zeros((SC, per_device), BF)
     stack[...] = jnp.zeros_like(stack)
 
     def add(sources):
-        s_parts, w_parts = [], []
+        r_parts, w_parts = [], []
         for src in sources:
             cell = cells_in[src]
-            s_parts.append((cell_at == cell // RC).astype(F32).astype(BF))
-            r_hot = (cell_at == cell % RC).astype(F32).astype(BF)
+            r_parts.append(jnp.where(cell_at == (cell % RC).astype(F32).astype(BF), one, none))
+            s_hot = jnp.where(cell_at == (cell // RC).astype(F32).astype(BF), one, none)
             values = recv[src]
             w_parts.append(
                 jnp.concatenate(
-                    [r_hot * values[m : m + 1, :] for m in range(channels)] + [r_hot],
+                    [s_hot * values[m : m + 1, :] for m in range(channels)] + [s_hot],
                     axis=0,
                 )
             )
         stack[...] += lax.dot_general(
-            jnp.concatenate(s_parts, axis=1),
             jnp.concatenate(w_parts, axis=1),
+            jnp.concatenate(r_parts, axis=1),
             NT_DIMS,
             preferred_element_type=F32,
         )
@@ -201,9 +203,9 @@
 
     lax.fori_loop(0, n // GROUP, add_step, 0)
 
-    scale = 1.0 / jnp.maximum(stack[:, channels * RC :], 1.0)
+    scale = 1.0 / jnp.maximum(stack[channels * SC :], 1.0)
     for m in range(channels):
-        out_ref[m // 2, m % 2] = stack[:, m * RC : (m + 1) * RC] * scale
+        out_ref[m // 2, m % 2] = stack[m * SC : (m + 1) * SC] * scale
 
     def drain(i, carry):
         peer = lax.rem(me + i, n)
@@ -239,7 +241,7 @@
             pltpu.VMEM((n, 1, local_traces), jnp.int32),
             pltpu.VMEM((n, channels, local_traces), BF),
             pltpu.VMEM((n, channels, local_traces), BF),
-            pltpu.VMEM((SC, (channels + 1) * RC), F32),
+            pltpu.VMEM(((channels + 1) * SC, RC), F32),
             pltpu.SemaphoreType.DMA((4,)),
             pltpu.SemaphoreType.DMA((PIECES,)),
             pltpu.SemaphoreType.DMA((n,)),

time: 14.7 us -> 14.2 us (0.966)
  Pallas kernels: 13.8 us -> 13.4 us
    pallas_call x1, Pallas kernels: 13.8 us -> 13.4 us  [local(): pl.pallas_call(functools.partial(kernel, n), out_shape=pltpu.VMEM((own_sl...]
where the time goes in v5:
time: 14.2 us; the launch traced here: 14.1 us
  Pallas kernels  13.4 us (94%)
  local copies, waits for them, and re-layouts  0.71 us (5%)
    pallas_call x1, Pallas kernels, local(): pl.pallas_call(functools.partial(kernel, n), out_shape=pltpu.VMEM((own_sl...  13.4 us
    unnamed x1, local copies, waits for them, and re-layouts  0.71 us

profile of v5, /device:TPU:0, one launch (start us, length us, event | category | flops | bytes accessed | tf_op | source)
XLA Modules:
  0.0 14.1 jit_solution(5207246016653798127)
XLA Ops:
  0.0 13.4 %shard_map.55 = f32[2,2,128,128]{3,2,1,0:T(8,128)S(1)} custom-call(bf16[512,4096]{1,0:T(8,128)(2,1)} %traces_hbm.1, s32[1,512]{1,0:T(1,128)} %bitcast.3, s32[1,512]{1,0:T(1,128)} %bitcast.4, s32[1,32]{1,0:T(1,128)} %bitcast.5, bf16[64,4096]{1,0:T(8,128)(2,1)} %constant.2.clone.table_hbm), custom_call_target="tpu_custom_call" | custom-call | tf_op jit(solution)/shard_map/pallas_call | solution.py:228
  13.4 0.7 %copy.7 = f32[2,2,128,128]{3,2,1,0:T(8,128)} copy(f32[2,2,128,128]{3,2,1,0:T(8,128)S(1)} %shard_map.55) | data formatting | bytes 524288

commit v6 on v5

--- a/solution.py
+++ b/solution.py
@@ -63,6 +63,14 @@
     rows, samples_count = table.shape
     channels = send.shape[1]
 
+    barrier = pltpu.get_barrier_semaphore()
+
+    def greet(i, carry):
+        pl.semaphore_signal(barrier, inc=1, device_id={"row": lax.rem(me + i, n)})
+        return carry
+
+    lax.fori_loop(1, n, greet, 0)
+
     def load(at, src, dst):
         return pltpu.make_async_copy(src, dst, load_sem.at[at])
 
@@ -72,7 +80,7 @@
         load(2, order_hbm, order),
         load(3, table_hbm, table),
     ]
-    for copy in loads:
+    for copy in loads[:3]:
         copy.start()
     trace_loads = [
         pltpu.make_async_copy(
@@ -80,16 +88,10 @@
         )
         for c in range(PIECES)
     ]
-    for copy in trace_loads:
+    trace_loads[0].start()
+    loads[3].start()
+    for copy in trace_loads[1:]:
         copy.start()
-
-    barrier = pltpu.get_barrier_semaphore()
-
-    def greet(i, carry):
-        pl.semaphore_signal(barrier, inc=1, device_id={"row": lax.rem(me + i, n)})
-        return carry
-
-    lax.fori_loop(1, n, greet, 0)
 
     loads[0].wait()
     loads[1].wait()

time: 14.2 us -> 14.3 us (level)
  no operation moved by 1% of the time
where the time goes in v6:
time: 14.3 us; the launch traced here: 14.2 us
  Pallas kernels  13.5 us (94%)
  local copies, waits for them, and re-layouts  0.71 us (5%)
    pallas_call x1, Pallas kernels, local(): pl.pallas_call(functools.partial(kernel, n), out_shape=pltpu.VMEM((own_sl...  13.5 us
    unnamed x1, local copies, waits for them, and re-layouts  0.71 us

profile of v6, /device:TPU:0, one launch (start us, length us, event | category | flops | bytes accessed | tf_op | source)
XLA Modules:
  0.0 14.2 jit_solution(15067888639893590066)
XLA Ops:
  0.0 13.5 %shard_map.55 = f32[2,2,128,128]{3,2,1,0:T(8,128)S(1)} custom-call(bf16[512,4096]{1,0:T(8,128)(2,1)} %traces_hbm.1, s32[1,512]{1,0:T(1,128)} %bitcast.3, s32[1,512]{1,0:T(1,128)} %bitcast.4, s32[1,32]{1,0:T(1,128)} %bitcast.5, bf16[64,4096]{1,0:T(8,128)(2,1)} %constant.2.clone.table_hbm), custom_call_target="tpu_custom_call" | custom-call | tf_op jit(solution)/shard_map/pallas_call | solution.py:230
  13.5 0.7 %copy.7 = f32[2,2,128,128]{3,2,1,0:T(8,128)} copy(f32[2,2,128,128]{3,2,1,0:T(8,128)S(1)} %shard_map.55) | data formatting | bytes 524288

commit v7 on v6

--- a/solution.py
+++ b/solution.py
@@ -181,11 +181,9 @@
                     axis=0,
                 )
             )
-        stack[...] += lax.dot_general(
-            jnp.concatenate(w_parts, axis=1),
-            jnp.concatenate(r_parts, axis=1),
-            NT_DIMS,
-            preferred_element_type=F32,
+        stack[...] += sum(
+            lax.dot_general(w, r, NT_DIMS, preferred_element_type=F32)
+            for w, r in zip(w_parts, r_parts)
         )
 
     own_cells.wait()

time: 14.3 us -> 14.3 us (level)
  no operation moved by 1% of the time
where the time goes in v7:
time: 14.3 us; the launch traced here: 14.2 us
  Pallas kernels  13.5 us (94%)
  local copies, waits for them, and re-layouts  0.71 us (5%)
    pallas_call x1, Pallas kernels, local(): pl.pallas_call(functools.partial(kernel, n), out_shape=pltpu.VMEM((own_sl...  13.5 us
    unnamed x1, local copies, waits for them, and re-layouts  0.71 us

profile of v7, /device:TPU:0, one launch (start us, length us, event | category | flops | bytes accessed | tf_op | source)
XLA Modules:
  0.0 14.2 jit_solution(15297767782921830431)
XLA Ops:
  0.0 13.5 %shard_map.55 = f32[2,2,128,128]{3,2,1,0:T(8,128)S(1)} custom-call(bf16[512,4096]{1,0:T(8,128)(2,1)} %traces_hbm.1, s32[1,512]{1,0:T(1,128)} %bitcast.3, s32[1,512]{1,0:T(1,128)} %bitcast.4, s32[1,32]{1,0:T(1,128)} %bitcast.5, bf16[64,4096]{1,0:T(8,128)(2,1)} %constant.2.clone.table_hbm), custom_call_target="tpu_custom_call" | custom-call | tf_op jit(solution)/shard_map/pallas_call | solution.py:228
  13.5 0.7 %copy.7 = f32[2,2,128,128]{3,2,1,0:T(8,128)} copy(f32[2,2,128,128]{3,2,1,0:T(8,128)S(1)} %shard_map.55) | data formatting | bytes 524288
